TPU v7x, 32 devices: a whole 2x2x4 slice. The times are simulated.
32 devices in a mesh: dp: 4 (over y, x), seq: 2 (over core), head: 4 (over z).
Axes of the slice: x: 2, y: 2, z: 4, core: 2. Of those that a mesh axis runs over, the one named last changes fastest.
Arguments:
- q_lat: bfloat16 [3072, 8192], P(('dp', 'seq'), 'head'), may hold values from -160 to 160
- q_rope: bfloat16 [3072, 1024], P(('dp', 'seq'), 'head'), may hold values from -6 to 6
- grad_out: bfloat16 [3072, 8192], P(('dp', 'seq'), 'head'), may hold values from -6 to 6
- prefix_keys: bfloat16 [576, 512], P(None, 'seq'), may hold values from -6 to 6
- comp_lengths: int32 [3], replicated, may hold values from 128 to 1024, as said below
- prefix_len: int32 [1], replicated, may hold values from 65 to 512
Outputs:
- dq_lat: bfloat16 [3072, 8192], P(('dp', 'seq'), 'head')
- dq_rope: bfloat16 [3072, 1024], P(('dp', 'seq'), 'head')
- d_keys: float32 [576, 512], P(None, ('seq', 'head'))
Inputs may be any that keep to these rules, and one draw needn't show every extreme that they name: `comp_lengths`: each a multiple of 128.
All inputs are finite; a program needn't handle non-finite values.
Results may differ from a plain program's by a relative error of at most 0.0089.
Values may be sent and summed in bfloat16 or wider, within the bound.
A program may use at most 64 MiB of HBM per device.

v0:
```python
import jax
import jax.numpy as jnp
from jax import lax
from jax.sharding import PartitionSpec as P

DL = 512
DR = 64
CLEN = 1024
neg_value = -1e30


def on_device(q_lat, q_rope, grad_out, prefix_keys, comp_lengths, prefix_len):
    tok_rows = q_lat.shape[0]
    heads_here = q_lat.shape[1] // DL
    rows = tok_rows * heads_here
    scale = (DL + DR) ** (-0.5)
    tok_ids = lax.axis_index(("dp", "seq")) * tok_rows + jnp.arange(tok_rows, dtype=jnp.int32)
    comp_ids = tok_ids // CLEN
    table = jnp.arange(comp_lengths.shape[0], dtype=jnp.int32)
    length = jnp.sum(
        jnp.where(comp_ids[:, None] == table[None, :], comp_lengths[None, :], 0), axis=1
    )
    valid = tok_ids % CLEN < length
    query_lat = q_lat.reshape(rows, DL)
    query_rope = q_rope.reshape(rows, DR)
    upstream = jnp.where(
        jnp.repeat(valid, heads_here)[:, None],
        grad_out.reshape(rows, DL),
        jnp.zeros((), jnp.bfloat16),
    )
    limit = prefix_len[0]
    total_keys = prefix_keys.shape[1] * lax.axis_size("seq")
    contract_last = (((1,), (1,)), ((), ()))
    contract_first = (((0,), (0,)), ((), ()))

    def scores_of(piece):
        key_lat = piece[:DL]
        key_rope = piece[DL:]
        scores = (
            jnp.dot(query_lat, key_lat, preferred_element_type=jnp.float32)
            + jnp.dot(query_rope, key_rope, preferred_element_type=jnp.float32)
        ) * scale
        keep = jnp.arange(piece.shape[1], dtype=jnp.int32) < limit
        dprob = jnp.dot(upstream, key_lat, preferred_element_type=jnp.float32)
        return (key_lat, key_rope, scores, keep[None, :], dprob)

    def make_backward(peak, total, delta):

        def backward_step(carry, piece, start):
            key_lat, key_rope, scores, keep, dprob = scores_of(piece)
            prob = jnp.where(
                keep,
                jnp.exp(jnp.where(keep, scores, neg_value) - peak[:, None]) / total[:, None],
                0.0,
            )
            dscore = prob * (dprob - delta[:, None])
            prob_b = prob.astype(jnp.bfloat16)
            dscore_b = dscore.astype(jnp.bfloat16)
            grad_lat = lax.dot_general(
                dscore_b, key_lat, contract_last, preferred_element_type=jnp.float32
            )
            grad_rope = lax.dot_general(
                dscore_b, key_rope, contract_last, preferred_element_type=jnp.float32
            )
            term_lat = lax.dot_general(
                upstream, prob_b, contract_first, preferred_element_type=jnp.float32
            ) + scale * lax.dot_general(
                query_lat, dscore_b, contract_first, preferred_element_type=jnp.float32
            )
            term_rope = scale * lax.dot_general(
                query_rope, dscore_b, contract_first, preferred_element_type=jnp.float32
            )
            update = jnp.concatenate([term_lat, term_rope], axis=0)
            return (grad_lat, grad_rope, update)

        return backward_step

    grads_init = (
        jnp.zeros((rows, DL), jnp.float32),
        jnp.zeros((rows, DR), jnp.float32),
        jnp.zeros((DL + DR, total_keys), jnp.float32),
    )
    peak = jnp.full((rows,), neg_value, jnp.float32)
    total = jnp.zeros((rows,), jnp.float32)
    key_lat, key_rope, scores, keep, dprob = scores_of(
        lax.all_gather(prefix_keys, "seq", axis=1, tiled=True)
    )
    masked = jnp.where(keep, scores, neg_value)
    new_peak = jnp.maximum(peak, jnp.max(masked, axis=1))
    expo = jnp.where(keep, jnp.exp(masked - new_peak[:, None]), 0.0)
    peak = new_peak
    total = jnp.sum(expo, axis=1)
    weighted = jnp.sum(expo * dprob, axis=1)
    backward_step = make_backward(peak, total, weighted / total)
    grad_lat, grad_rope, key_grads = backward_step(
        grads_init, lax.all_gather(prefix_keys, "seq", axis=1, tiled=True), jnp.int32(0)
    )
    by_seq = lax.psum_scatter(key_grads, "seq", scatter_dimension=1, tiled=True)
    portion = lax.psum_scatter(by_seq, "head", scatter_dimension=1, tiled=True)
    d_keys = lax.psum(portion, "dp")
    dq_lat = (scale * grad_lat).astype(jnp.bfloat16).reshape(tok_rows, heads_here * DL)
    dq_rope = (scale * grad_rope).astype(jnp.bfloat16).reshape(tok_rows, heads_here * DR)
    return (dq_lat, dq_rope, d_keys)


def solution(mesh):
    in_specs = (
        P(("dp", "seq"), "head"),
        P(("dp", "seq"), "head"),
        P(("dp", "seq"), "head"),
        P(None, "seq"),
        P(),
        P(),
    )
    out_specs = (P(("dp", "seq"), "head"), P(("dp", "seq"), "head"), P(None, ("seq", "head")))
    return jax.shard_map(
        on_device, mesh=mesh, in_specs=in_specs, out_specs=out_specs, check_vma=False
    )
```

profile of v0, /device:TPU:0, one launch (start us, length us, event | category | flops | bytes accessed | tf_op | source)
XLA Modules:
  0.0 119.2 jit_solution(12004956962151974699)
XLA Ops:
  7.2 0.0 reduce-scatter.5.cloned.1.call-start
  7.9 0.7 select_reduce_fusion.1
  8.7 0.1 broadcast_in_dim.73
  8.8 0.2 broadcast_in_dim.74
  8.9 1.2 reshape.56
  10.1 2.6 %all_gather.4 = bf16[576,512]{1,0:T(8,128)(2,1)S(1)} all-gather(bf16[576,256]{1,0:T(8,128)(2,1)} %param.9), channel_id=1, replica_groups=mesh['dp'=4,'seq'=2,'head'=4] {'seq'}, dimensions={1}, use_global_device_ids=true | all-gather | bytes 884736 | tf_op jit(solution)/shard_map/all_gather | solution.py:96
  12.7 0.0 copy-start
  12.7 2.9 %reshape.55 = bf16[1536,512]{1,0:T(8,128)(2,1)S(1)} reshape(bf16[384,2048]{1,0:T(8,128)(2,1)} %param.6) | data formatting | bytes 3145728 | tf_op jit(solution)/shard_map/reshape | solution.py:24
  15.6 3.7 %reshape.57 = bf16[1536,512]{1,0:T(8,128)(2,1)} reshape(bf16[384,2048]{1,0:T(8,128)(2,1)} %param.8) | data formatting | bytes 3145728 | tf_op jit(solution)/shard_map/reshape | solution.py:28
  19.4 1.0 fusion.12
  20.4 0.0 copy-start.2
  20.4 0.7 fusion.22
  21.2 0.0 copy-done
  21.2 0.6 copy-done.2
  21.8 1.6 %select_reduce_fusion = (f32[1536]{0:T(1024)S(1)}, f32[1536]{0:T(1024)S(1)}, f32[1536,512]{0,1:T(8,128)S(1)}) fusion(f32[1536,512]{0,1:T(8,128)S(1)} %get-tuple-element.18, f32[1536]{0:T(1024)S(1)} %broadcast_maximum_fusion, pred[512]{0:T(512)(128)(4,1)S(1)} %iota_compare_fusion.1, bf16[576,512]{1,0:T(8,128)(2,1)S(1)} %all_gather.4, ...), kind=kOutput, calls=%fused_computation.9 | convolution fusion | flops 810021888 | bytes 8411648 | tf_op jit(solution)/shard_map/dot_general | solution.py:44
  23.4 1.5 %fusion.4 = f32[512,512]{1,0:T(8,128)S(1)} fusion(bf16[1536,512]{1,0:T(8,128)(2,1)S(1)} %copy-done.2, pred[1536]{0:T(1024)(128)(4,1)S(1)} %broadcast_in_dim.74, f32[1536,512]{0,1:T(8,128)S(1)} %get-tuple-element.18, f32[1536]{0:T(1024)S(1)} %get-tuple-element.15, f32[1536]{0:T(1024)S(1)} %broadcast_maximum_fusion, pred[512]{0:T(512)(128)(4,1)S(1)} %iota_compare_fusion.1), kind=kOutput, calls=%fused_computation.12 | convolution fusion | flops 809238528 | bytes 5781504 | tf_op jit(solution)/shard_map/dot_general | solution.py:65
  24.9 0.9 multiply_convert_fusion
  25.8 0.6 fusion.8
  26.4 1.0 fusion.7
  27.4 1.1 pad_maximum_fusion
  28.5 0.0 copy-start.1
  28.5 0.0 reduce-scatter.5.cloned.1.call-update
  28.5 0.0 reduce-scatter.7.cloned.1.call-start
  28.6 11.2 %reduce-scatter.5.cloned.1.call-done = f32[576,256]{1,0:T(8,128)} async-done(((f32[576,512]{1,0:T(8,128)}), f32[576,256]{1,0:T(8,128)}) %reduce-scatter.5.cloned.1.call-update) | async-done | bytes 589840 | tf_op jit(solution)/shard_map/reduce_scatter | solution.py:98
  39.8 2.1 %copy.24 = f32[576,256]{0,1:T(8,128)} copy(f32[576,256]{1,0:T(8,128)} %reduce-scatter.5.cloned.1.call-done) | data formatting | bytes 1179648
  41.9 0.0 reduce-scatter.7.cloned.1.call-update
  41.9 0.0 all-reduce.2.cloned.1.call-start
  42.0 0.0 copy-done.1
  42.0 2.1 %fusion.2 = bf16[1536,512]{0,1:T(8,128)(2,1)} fusion(bf16[1536,512]{0,1:T(8,128)(2,1)S(1)} %multiply_convert_fusion, bf16[576,512]{1,0:T(8,128)(2,1)S(1)} %copy-done.1), kind=kOutput, calls=%fused_computation.8 | convolution fusion | flops 806879232 | bytes 3670016 | tf_op jit(solution)/shard_map/dot_general | solution.py:59
  44.1 1.7 %copy.20 = bf16[1536,512]{1,0:T(8,128)(2,1)S(1)} copy(bf16[1536,512]{0,1:T(8,128)(2,1)} %fusion.2) | data formatting | bytes 3145728 | tf_op jit(solution)/shard_map/convert_element_type | solution.py:101
  45.8 2.2 %reshape.58 = bf16[384,2048]{1,0:T(8,128)(2,1)} reshape(bf16[1536,512]{1,0:T(8,128)(2,1)S(1)} %copy.20) | data formatting | bytes 3145728 | tf_op jit(solution)/shard_map/reshape | solution.py:101
  48.1 17.8 %reduce-scatter.7.cloned.1.call-done = f32[64,576]{1,0:T(8,128)} async-done(((f32[256,576]{1,0:T(8,128)}), f32[64,576]{1,0:T(8,128)}) %reduce-scatter.7.cloned.1.call-update) | async-done | bytes 147472
  65.9 1.8 %copy.25 = f32[576,64]{1,0:T(8,128)} copy(f32[576,64]{0,1:T(8,128)} %bitcast.19) | data formatting | bytes 294912
  67.7 0.0 all-reduce.2.cloned.1.call-update
  67.7 1.2 %fusion.3 = bf16[1536,64]{0,1:T(8,128)(2,1)S(1)} fusion(bf16[1536,512]{0,1:T(8,128)(2,1)S(1)} %multiply_convert_fusion, bf16[576,512]{1,0:T(8,128)(2,1)} %copy-done), kind=kOutput, calls=%fused_computation.11 | convolution fusion | flops 100859904 | bytes 1835008 | tf_op jit(solution)/shard_map/dot_general | solution.py:62
  68.9 0.2 copy.21
  69.2 1.0 reshape.59
  70.1 40.8 %all-reduce.2.cloned.1.call-done = f32[576,64]{1,0:T(8,128)} async-done(((f32[576,64]{1,0:T(8,128)}), f32[576,64]{1,0:T(8,128)}) %all-reduce.2.cloned.1.call-update) | async-done | bytes 147472 | tf_op jit(solution)/shard_map/psum | solution.py:100
  110.9 1.8 %copy.22 = f32[576,64]{0,1:T(8,128)} copy(f32[576,64]{1,0:T(8,128)} %all-reduce.2.cloned.1.call-done) | data formatting | bytes 294912
  (5 shorter events, 0.0 us)
Async XLA Ops:
  7.2 32.6 %reduce-scatter.5.cloned.1.call-start = ((), (), s32[]{:S(2)}) async-start(), calls=%async_computation.2 | async-start | bytes 1769472 | tf_op jit(solution)/shard_map/reduce_scatter | solution.py:98
  12.7 8.5 %copy-start = (bf16[576,512]{1,0:T(8,128)(2,1)}, bf16[576,512]{1,0:T(8,128)(2,1)S(1)}, u32[]{:S(2)}) copy-start(bf16[576,512]{1,0:T(8,128)(2,1)S(1)} %all_gather.4) | copy-start | bytes 1769476
  20.4 1.4 %copy-start.2 = (bf16[1536,512]{1,0:T(8,128)(2,1)S(1)}, bf16[1536,512]{1,0:T(8,128)(2,1)}, u32[]{:S(2)}) copy-start(bf16[1536,512]{1,0:T(8,128)(2,1)} %reshape.57) | copy-start | bytes 4718596
  28.5 13.5 %copy-start.1 = (bf16[576,512]{1,0:T(8,128)(2,1)S(1)}, bf16[576,512]{1,0:T(8,128)(2,1)}, u32[]{:S(2)}) copy-start(bf16[576,512]{1,0:T(8,128)(2,1)} %copy-done) | copy-start | bytes 1769476
  28.5 37.4 %reduce-scatter.7.cloned.1.call-start = ((), (), s32[]{:S(2)}) async-start(), calls=%async_computation.4 | async-start | bytes 819200
  41.9 69.0 %all-reduce.2.cloned.1.call-start = ((), (), s32[]{:S(2)}) async-start(), calls=%async_computation.3 | async-start | bytes 589824 | tf_op jit(solution)/shard_map/psum | solution.py:100
Sparse Core Ops, SparseCore 0:
  28.6 11.0 reduce-scatter.4
  42.1 23.8 reduce-scatter.6
  68.9 41.9 all-reduce.1
where the time goes:
time: 120 us; the launch traced here: 119 us
  waiting for transfers between devices  69.9 us (58%)
  local copies, waits for them, and re-layouts  19.6 us (16%)
  between operations  14.5 us (12%)
  matrix products  9.83 us (8%)
  other arithmetic  2.74 us (2%)
  blocking collectives  2.56 us (2%)
    psum x1, waiting for transfers between devices, on_device(): d_keys = lax.psum(portion, 'dp')  40.8 us
    unnamed x4, waiting for transfers between devices  17.9 us
    reduce_scatter x1, waiting for transfers between devices, on_device(): by_seq = lax.psum_scatter(key_grads, 'seq', scatter_dimension=1, tiled=True)  11.2 us
    unnamed x9, local copies, waits for them, and re-layouts  6.33 us
    reshape x1, local copies, waits for them, and re-layouts, on_device(): grad_out.reshape(rows, DL)  3.73 us
    reshape x1, local copies, waits for them, and re-layouts, on_device(): query_lat = q_lat.reshape(rows, DL)  2.94 us
    all_gather x1, blocking collectives, on_device(): lax.all_gather(prefix_keys, 'seq', axis=1, tiled=True)  2.56 us
  transfers between devices with their start and end apart: 3, of which 3 were waited for; matrix products, arithmetic and copies ran while one was open for 7% of the time, Pallas kernels for 0%

commit v1 on v0

--- a/solution.py
+++ b/solution.py
@@ -97,7 +97,8 @@
     )
     by_seq = lax.psum_scatter(key_grads, "seq", scatter_dimension=1, tiled=True)
     portion = lax.psum_scatter(by_seq, "head", scatter_dimension=1, tiled=True)
-    d_keys = lax.psum(portion, "dp")
+    parts = lax.all_gather(portion, "dp", axis=0, tiled=False)
+    d_keys = parts.sum(axis=0)
     dq_lat = (scale * grad_lat).astype(jnp.bfloat16).reshape(tok_rows, heads_here * DL)
     dq_rope = (scale * grad_rope).astype(jnp.bfloat16).reshape(tok_rows, heads_here * DR)
     return (dq_lat, dq_rope, d_keys)

time: 120 us -> 86.6 us (0.72)
  waiting for transfers between devices: 69.9 us -> 26.7 us
  blocking collectives: 2.56 us -> 14 us
  local copies, waits for them, and re-layouts: 19.6 us -> 17.2 us
    psum x1 -> x0, waiting for transfers between devices: 40.8 us -> none  [on_device(): d_keys = lax.psum(portion, 'dp')]
    all_gather x0 -> x1, blocking collectives: none -> 11.4 us  [on_device(): parts = lax.all_gather(portion, 'dp', axis=0, tiled=False)]
    unnamed x4 -> x3, waiting for transfers between devices: 17.9 us -> 15.5 us
    unnamed x9, local copies, waits for them, and re-layouts: 6.33 us -> 3.98 us
  transfers between devices with their start and end apart: 3 -> 2, of which waited for: 3 -> 2; matrix products, arithmetic and copies ran while one was open for 7% -> 10% of each run, Pallas kernels for 0% -> 0%
where the time goes in v1:
time: 86.6 us; the launch traced here: 86.1 us
  waiting for transfers between devices  26.7 us (31%)
  local copies, waits for them, and re-layouts  17.2 us (20%)
  between operations  14.8 us (17%)
  blocking collectives  14 us (16%)
  matrix products  9.83 us (11%)
  other arithmetic  3.44 us (4%)
    unnamed x3, waiting for transfers between devices  15.5 us
    all_gather x1, blocking collectives, on_device(): parts = lax.all_gather(portion, 'dp', axis=0, tiled=False)  11.4 us
    reduce_scatter x1, waiting for transfers between devices, on_device(): by_seq = lax.psum_scatter(key_grads, 'seq', scatter_dimension=1, tiled=True)  11.2 us
    unnamed x9, local copies, waits for them, and re-layouts  3.98 us
    reshape x1, local copies, waits for them, and re-layouts, on_device(): grad_out.reshape(rows, DL)  3.73 us
    reshape x1, local copies, waits for them, and re-layouts, on_device(): query_lat = q_lat.reshape(rows, DL)  2.94 us
    all_gather x1, blocking collectives, on_device(): lax.all_gather(prefix_keys, 'seq', axis=1, tiled=True)  2.56 us
    reshape x1, local copies, waits for them, and re-layouts, on_device(): (scale * grad_lat).astype(jnp.bfloat16).reshape(tok_rows, heads_here * DL)  2.23 us
  transfers between devices with their start and end apart: 2, of which 2 were waited for; matrix products, arithmetic and copies ran while one was open for 10% of the time, Pallas kernels for 0%

profile of v1, /device:TPU:0, one launch (start us, length us, event | category | flops | bytes accessed | tf_op | source)
XLA Modules:
  0.0 86.1 jit_solution(5987256369145521647)
XLA Ops:
  7.2 0.0 reduce-scatter.5.cloned.1.call-start
  7.9 0.7 select_reduce_fusion.1
  8.7 0.1 broadcast_in_dim.73
  8.8 0.2 broadcast_in_dim.74
  8.9 1.2 %reshape.56 = bf16[1536,64]{1,0:T(8,128)(2,1)S(1)} reshape(bf16[384,256]{1,0:T(8,128)(2,1)} %param.7) | data formatting | bytes 393216 | tf_op jit(solution)/shard_map/reshape | solution.py:25
  10.1 2.6 %all_gather.10 = bf16[576,512]{1,0:T(8,128)(2,1)S(1)} all-gather(bf16[576,256]{1,0:T(8,128)(2,1)} %param.9), channel_id=1, replica_groups=mesh['dp'=4,'seq'=2,'head'=4] {'seq'}, dimensions={1}, use_global_device_ids=true | all-gather | bytes 884736 | tf_op jit(solution)/shard_map/all_gather | solution.py:96
  12.7 0.0 copy-start
  12.7 2.9 %reshape.55 = bf16[1536,512]{1,0:T(8,128)(2,1)S(1)} reshape(bf16[384,2048]{1,0:T(8,128)(2,1)} %param.6) | data formatting | bytes 3145728 | tf_op jit(solution)/shard_map/reshape | solution.py:24
  15.6 3.7 %reshape.57 = bf16[1536,512]{1,0:T(8,128)(2,1)} reshape(bf16[384,2048]{1,0:T(8,128)(2,1)} %param.8) | data formatting | bytes 3145728 | tf_op jit(solution)/shard_map/reshape | solution.py:28
  19.4 1.0 %fusion.12 = f32[1536,512]{0,1:T(8,128)S(1)} fusion(bf16[1536,512]{1,0:T(8,128)(2,1)S(1)} %reshape.55, bf16[576,512]{1,0:T(8,128)(2,1)S(1)} %all_gather.10), kind=kOutput, calls=%fused_computation.24 | convolution fusion | flops 805306368 | bytes 5242880 | tf_op jit(solution)/shard_map/dot_general | solution.py:40
  20.4 0.0 copy-start.2
  20.4 0.7 fusion.22
  21.2 0.0 copy-done
  21.2 0.6 copy-done.2
  21.8 1.6 %select_reduce_fusion = (f32[1536]{0:T(1024)S(1)}, f32[1536]{0:T(1024)S(1)}, f32[1536,512]{0,1:T(8,128)S(1)}) fusion(f32[1536,512]{0,1:T(8,128)S(1)} %get-tuple-element.12, f32[1536]{0:T(1024)S(1)} %broadcast_maximum_fusion, pred[512]{0:T(512)(128)(4,1)S(1)} %iota_compare_fusion.1, bf16[576,512]{1,0:T(8,128)(2,1)S(1)} %all_gather.10, ...), kind=kOutput, calls=%fused_computation.9 | convolution fusion | flops 810021888 | bytes 8411648 | tf_op jit(solution)/shard_map/dot_general | solution.py:44
  23.4 1.5 %fusion.4 = f32[512,512]{1,0:T(8,128)S(1)} fusion(bf16[1536,512]{1,0:T(8,128)(2,1)S(1)} %copy-done.2, pred[1536]{0:T(1024)(128)(4,1)S(1)} %broadcast_in_dim.74, f32[1536,512]{0,1:T(8,128)S(1)} %get-tuple-element.12, f32[1536]{0:T(1024)S(1)} %get-tuple-element.9, f32[1536]{0:T(1024)S(1)} %broadcast_maximum_fusion, pred[512]{0:T(512)(128)(4,1)S(1)} %iota_compare_fusion.1), kind=kOutput, calls=%fused_computation.12 | convolution fusion | flops 809238528 | bytes 5781504 | tf_op jit(solution)/shard_map/dot_general | solution.py:65
  24.9 0.9 multiply_convert_fusion
  25.8 0.6 fusion.8
  26.4 1.0 %fusion.7 = f32[512,512]{1,0:T(8,128)S(1)} fusion(f32[512,512]{1,0:T(8,128)S(1)} %fusion.4, bf16[1536,512]{0,1:T(8,128)(2,1)S(1)} %multiply_convert_fusion, bf16[1536,512]{1,0:T(8,128)(2,1)S(1)} %reshape.55), kind=kOutput, calls=%fused_computation.17 | convolution fusion | flops 805830656 | bytes 5242880 | tf_op jit(solution)/shard_map/dot_general | solution.py:67
  27.4 1.1 %pad_maximum_fusion = f32[576,512]{1,0:T(8,128)} fusion(f32[64,512]{1,0:T(8,128)S(1)} %fusion.8, f32[512,512]{1,0:T(8,128)S(1)} %fusion.7), kind=kLoop, calls=%fused_computation.18 | loop fusion | flops 294912 | bytes 2359296 | tf_op jit(solution)/shard_map/concatenate | solution.py:73
  28.5 0.0 copy-start.1
  28.5 0.0 reduce-scatter.5.cloned.1.call-update
  28.5 0.0 reduce-scatter.7.cloned.1.call-start
  28.6 11.2 %reduce-scatter.5.cloned.1.call-done = f32[576,256]{1,0:T(8,128)} async-done(((f32[576,512]{1,0:T(8,128)}), f32[576,256]{1,0:T(8,128)}) %reduce-scatter.5.cloned.1.call-update) | async-done | bytes 589840 | tf_op jit(solution)/shard_map/reduce_scatter | solution.py:98
  39.8 2.1 %copy.26 = f32[576,256]{0,1:T(8,128)} copy(f32[576,256]{1,0:T(8,128)} %reduce-scatter.5.cloned.1.call-done) | data formatting | bytes 1179648
  41.9 0.0 reduce-scatter.7.cloned.1.call-update
  41.9 0.0 copy-done.1
  41.9 2.1 %fusion.2 = bf16[1536,512]{0,1:T(8,128)(2,1)} fusion(bf16[1536,512]{0,1:T(8,128)(2,1)S(1)} %multiply_convert_fusion, bf16[576,512]{1,0:T(8,128)(2,1)S(1)} %copy-done.1), kind=kOutput, calls=%fused_computation.8 | convolution fusion | flops 806879232 | bytes 3670016 | tf_op jit(solution)/shard_map/dot_general | solution.py:59
  44.1 1.7 %copy.20 = bf16[1536,512]{1,0:T(8,128)(2,1)S(1)} copy(bf16[1536,512]{0,1:T(8,128)(2,1)} %fusion.2) | data formatting | bytes 3145728 | tf_op jit(solution)/shard_map/convert_element_type | solution.py:102
  45.8 2.2 %reshape.58 = bf16[384,2048]{1,0:T(8,128)(2,1)} reshape(bf16[1536,512]{1,0:T(8,128)(2,1)S(1)} %copy.20) | data formatting | bytes 3145728 | tf_op jit(solution)/shard_map/reshape | solution.py:102
  48.0 1.2 %fusion.3 = bf16[1536,64]{0,1:T(8,128)(2,1)S(1)} fusion(bf16[1536,512]{0,1:T(8,128)(2,1)S(1)} %multiply_convert_fusion, bf16[576,512]{1,0:T(8,128)(2,1)} %copy-done), kind=kOutput, calls=%fused_computation.11 | convolution fusion | flops 100859904 | bytes 1835008 | tf_op jit(solution)/shard_map/dot_general | solution.py:62
  49.2 0.2 copy.21
  49.5 1.0 %reshape.59 = bf16[384,256]{1,0:T(8,128)(2,1)} reshape(bf16[1536,64]{1,0:T(8,128)(2,1)S(1)} %copy.21) | data formatting | bytes 393216 | tf_op jit(solution)/shard_map/reshape | solution.py:103
  50.4 15.5 %reduce-scatter.7.cloned.1.call-done = f32[64,576]{1,0:T(8,128)} async-done(((f32[256,576]{1,0:T(8,128)}), f32[64,576]{1,0:T(8,128)}) %reduce-scatter.7.cloned.1.call-update) | async-done | bytes 147472
  65.9 1.1 %copy.27 = f32[576,64]{1,0:T(8,128)S(1)} copy(f32[576,64]{0,1:T(8,128)} %bitcast.21) | data formatting | bytes 294912
  67.0 0.1 copy.22
  67.1 11.4 %all-gather.1 = f32[4,576,64]{1,2,0:T(8,128)S(1)} all-gather(f32[1,576,64]{1,2,0:T(8,128)S(1)} %copy.22), channel_id=2, replica_groups=mesh['dp'=4,'seq'=2,'head'=4] {'dp'}, dimensions={0}, use_global_device_ids=true | all-gather | bytes 737280 | tf_op jit(solution)/shard_map/all_gather | solution.py:100
  78.5 0.7 reduce_sum.39
  (5 shorter events, 0.0 us)
Async XLA Ops:
  7.2 32.6 %reduce-scatter.5.cloned.1.call-start = ((), (), s32[]{:S(2)}) async-start(), calls=%async_computation.2 | async-start | bytes 1769472 | tf_op jit(solution)/shard_map/reduce_scatter | solution.py:98
  12.7 8.5 %copy-start = (bf16[576,512]{1,0:T(8,128)(2,1)}, bf16[576,512]{1,0:T(8,128)(2,1)S(1)}, u32[]{:S(2)}) copy-start(bf16[576,512]{1,0:T(8,128)(2,1)S(1)} %all_gather.10) | copy-start | bytes 1769476
  20.4 1.4 %copy-start.2 = (bf16[1536,512]{1,0:T(8,128)(2,1)S(1)}, bf16[1536,512]{1,0:T(8,128)(2,1)}, u32[]{:S(2)}) copy-start(bf16[1536,512]{1,0:T(8,128)(2,1)} %reshape.57) | copy-start | bytes 4718596
  28.5 13.4 %copy-start.1 = (bf16[576,512]{1,0:T(8,128)(2,1)S(1)}, bf16[576,512]{1,0:T(8,128)(2,1)}, u32[]{:S(2)}) copy-start(bf16[576,512]{1,0:T(8,128)(2,1)} %copy-done) | copy-start | bytes 1769476
  28.5 37.4 %reduce-scatter.7.cloned.1.call-start = ((), (), s32[]{:S(2)}) async-start(), calls=%async_computation.3 | async-start | bytes 819200
Sparse Core Ops, SparseCore 0:
  28.6 11.0 reduce-scatter.4
  42.1 23.8 reduce-scatter.6
